TPU v7x, 32 devices: a whole 2x2x4 slice. The times are simulated.
32 devices in a mesh: row: 4 (over z), col: 8 (over y, x, core).
Axes of the slice: x: 2, y: 2, z: 4, core: 2. Of those that a mesh axis runs over, the one named last changes fastest.
Arguments:
- factor: bfloat16 [32768, 5, 1024], P('col', None, 'row'), may hold values from -0.0625 to 0.0625
- diag_inverse: bfloat16 [5, 1024, 1024], P(None, 'row'), may hold values from -1 to 2
- right_side: float32 [16, 32, 1024], P(None, 'col', 'row'), may hold values from -6 to 6
- tile_order: int32 [32], replicated, may hold values from 0 to 31, each once
- live_segments: int32 [16], replicated, may hold values from 2 to 5
Outputs:
- result: float32 [16, 32, 1024], P(None, 'col', 'row')
Inputs may be any that keep to these rules, and one draw needn't show every extreme that they name: `tile_order`: each of 0 to 31 appears once.
All inputs are finite; a program needn't handle non-finite values.
Results may differ from a plain program's by a relative error of at most 0.0019.
Values may be sent and summed in bfloat16 or wider, within the bound.
A program may use at most 64 MiB of HBM per device.

v0:
```python
import jax
import jax.numpy as jnp
from jax import lax
from jax.sharding import PartitionSpec as P


def spread(block, axis, owner):
    block = jnp.where(lax.axis_index(axis) == owner, block, jnp.zeros_like(block))
    return lax.psum(block, axis)


def per_device(factor, diag_inverse, right_side, tile_order, live_segments):
    section_count = diag_inverse.shape[0]
    slice_width = diag_inverse.shape[1]
    tile_width = diag_inverse.shape[2]
    rhs_count = right_side.shape[0]
    rows_dev = right_side.shape[1]
    my_col = lax.axis_index("col")
    my_row = lax.axis_index("row")
    slice_start = my_row * slice_width
    partial_value = jnp.zeros((rhs_count, rows_dev * tile_width), jnp.float32)
    result = jnp.zeros((rhs_count, rows_dev, slice_width), jnp.float32)
    for section in range(section_count):
        slot_id = tile_order[section]
        root_col = slot_id // rows_dev
        local_pos = slot_id % rows_dev
        part_tile = lax.dynamic_slice_in_dim(partial_value, local_pos * tile_width, tile_width, 1)
        rhs_slice = lax.dynamic_index_in_dim(right_side, local_pos, 1, keepdims=False)
        placed = lax.dynamic_update_slice_in_dim(
            jnp.zeros((rhs_count, tile_width), jnp.float32), rhs_slice, slice_start, 1
        )
        remaining = lax.psum(placed - part_tile, "row")
        inverse = diag_inverse[section].astype(jnp.float32)
        solved = lax.dot_general(
            remaining,
            inverse,
            (((1,), (1,)), ((), ())),
            precision=lax.Precision.HIGHEST,
            preferred_element_type=jnp.float32,
        )
        is_live = (section < live_segments)[:, None]
        sent_block = jnp.where(is_live, solved, jnp.zeros_like(solved)).astype(jnp.bfloat16)
        sent_block = spread(sent_block, "col", root_col)
        kept_part = lax.dynamic_slice_in_dim(remaining, slice_start, slice_width, 1)
        stored = jnp.where(is_live, solved, kept_part)
        written = lax.dynamic_update_slice_in_dim(result, stored[:, None, :], local_pos, 1)
        result = jnp.where(my_col == root_col, written, result)
        panel_rows = factor[:, section, :]
        partial_value = partial_value + lax.dot_general(
            sent_block, panel_rows, (((1,), (1,)), ((), ())), preferred_element_type=jnp.float32
        )
    shaped = partial_value.reshape(rhs_count, rows_dev, tile_width)
    total_part = lax.psum_scatter(shaped, "row", scatter_dimension=2, tiled=True)
    local_slots = my_col * rows_dev + jnp.arange(rows_dev, dtype=jnp.int32)
    visited = jnp.any(local_slots[:, None] == tile_order[:section_count][None, :], axis=1)
    return jnp.where(visited[None, :, None], result, right_side - total_part)


def solution(mesh):
    return jax.shard_map(
        per_device,
        mesh=mesh,
        in_specs=(P("col", None, "row"), P(None, "row", None), P(None, "col", "row"), P(), P()),
        out_specs=P(None, "col", "row"),
        check_vma=False,
    )
```

profile of v0, /device:TPU:0, one launch (start us, length us, event | category | flops | bytes accessed | tf_op | source)
XLA Modules:
  0.0 292.0 jit_solution(3287406973859240953)
XLA Ops:
  6.5 1.5 fusion.35
  10.1 0.9 copy.16
  22.0 26.9 %all-reduce.6.cloned.1.call-done = f32[16,1024]{1,0:T(8,128)} async-done(((f32[16,1024]{1,0:T(8,128)}), f32[16,1024]{1,0:T(8,128)}) %all-reduce.6.cloned.1.call-update) | async-done | bytes 65552 | tf_op jit(solution)/shard_map/psum | solution.py:32
  48.9 1.6 bitcast_dynamic-update-slice_fusion.4
  50.5 12.1 %psum.71 = bf16[16,256]{1,0:T(8,128)(2,1)S(1)} all-reduce(bf16[16,256]{1,0:T(8,128)(2,1)S(1)} %fusion.30), channel_id=1, replica_groups=mesh['row'=4,'col'=8] {'col'}, use_global_device_ids=true, to_apply=%region_2.3 | all-reduce | flops 4096 | bytes 16384 | tf_op jit(solution)/shard_map/psum | solution.py:9
  62.7 2.2 fusion.4
  65.7 33.1 %all-reduce.8.cloned.1.call-done = f32[16,1024]{1,0:T(8,128)} async-done(((f32[16,1024]{1,0:T(8,128)}), f32[16,1024]{1,0:T(8,128)}) %all-reduce.8.cloned.1.call-update) | async-done | bytes 65552 | tf_op jit(solution)/shard_map/psum | solution.py:32
  98.8 1.4 fusion.29
  100.3 12.1 %psum.73 = bf16[16,256]{1,0:T(8,128)(2,1)S(1)} all-reduce(bf16[16,256]{1,0:T(8,128)(2,1)S(1)} %fusion.31), channel_id=1, replica_groups=mesh['row'=4,'col'=8] {'col'}, use_global_device_ids=true, to_apply=%region_4.5 | all-reduce | flops 4096 | bytes 16384 | tf_op jit(solution)/shard_map/psum | solution.py:9
  112.4 2.2 convolution_add_fusion.3
  115.4 33.1 %all-reduce.10.cloned.1.call-done = f32[16,1024]{1,0:T(8,128)} async-done(((f32[16,1024]{1,0:T(8,128)}), f32[16,1024]{1,0:T(8,128)}) %all-reduce.10.cloned.1.call-update) | async-done | bytes 65552 | tf_op jit(solution)/shard_map/psum | solution.py:32
  148.5 1.4 fusion.28
  150.0 12.1 %psum.75 = bf16[16,256]{1,0:T(8,128)(2,1)S(1)} all-reduce(bf16[16,256]{1,0:T(8,128)(2,1)S(1)} %fusion.32), channel_id=1, replica_groups=mesh['row'=4,'col'=8] {'col'}, use_global_device_ids=true, to_apply=%region_6.7 | all-reduce | flops 4096 | bytes 16384 | tf_op jit(solution)/shard_map/psum | solution.py:9
  162.1 2.2 convolution_add_fusion.2
  165.1 33.1 %all-reduce.12.cloned.1.call-done = f32[16,1024]{1,0:T(8,128)} async-done(((f32[16,1024]{1,0:T(8,128)}), f32[16,1024]{1,0:T(8,128)}) %all-reduce.12.cloned.1.call-update) | async-done | bytes 65552 | tf_op jit(solution)/shard_map/psum | solution.py:32
  198.3 1.4 fusion.27
  199.7 12.1 %psum.77 = bf16[16,256]{1,0:T(8,128)(2,1)S(1)} all-reduce(bf16[16,256]{1,0:T(8,128)(2,1)S(1)} %fusion.33), channel_id=1, replica_groups=mesh['row'=4,'col'=8] {'col'}, use_global_device_ids=true, to_apply=%region_8.9 | all-reduce | flops 4096 | bytes 16384 | tf_op jit(solution)/shard_map/psum | solution.py:9
  211.9 2.2 convolution_add_fusion.1
  215.5 32.5 %all-reduce.14.cloned.1.call-done = f32[16,1024]{1,0:T(8,128)} async-done(((f32[16,1024]{1,0:T(8,128)}), f32[16,1024]{1,0:T(8,128)}) %all-reduce.14.cloned.1.call-update) | async-done | bytes 65552 | tf_op jit(solution)/shard_map/psum | solution.py:32
  248.0 1.4 fusion.26
  249.5 12.1 %psum.79 = bf16[16,256]{1,0:T(8,128)(2,1)S(1)} all-reduce(bf16[16,256]{1,0:T(8,128)(2,1)S(1)} %fusion.34), channel_id=1, replica_groups=mesh['row'=4,'col'=8] {'col'}, use_global_device_ids=true, to_apply=%region_10.11 | all-reduce | flops 4096 | bytes 16384 | tf_op jit(solution)/shard_map/psum | solution.py:9
  261.6 2.2 convolution_add_fusion
  264.8 18.8 %reduce-scatter.2.cloned.1.call-done = f32[16,4,256]{2,0,1:T(8,128)} async-done(((f32[16,4,1024]{2,0,1:T(8,128)}), f32[16,4,256]{2,0,1:T(8,128)}) %reduce-scatter.2.cloned.1.call-update) | async-done | bytes 65552 | tf_op jit(solution)/shard_map/reduce_scatter | solution.py:53
  283.5 0.9 subtract_select_fusion
  (45 shorter events, 6.3 us)
Async XLA Ops:
  6.5 92.3 %copy-start = (bf16[5,256,1024]{2,1,0:T(8,128)(2,1)S(1)}, bf16[5,256,1024]{2,1,0:T(8,128)(2,1)}, u32[]{:S(2)}) copy-start(bf16[5,256,1024]{2,1,0:T(8,128)(2,1)} %param.6) | copy-start | bytes 7864324
  6.5 42.3 %all-reduce.6.cloned.1.call-start = ((), (), s32[]{:S(2)}) async-start(), calls=%async_computation.1 | async-start | bytes 131072 | tf_op jit(solution)/shard_map/psum | solution.py:32
  11.0 0.6 copy-start.1
  11.7 87.1 %all-reduce.8.cloned.1.call-start = ((), (), s32[]{:S(2)}) async-start(), calls=%async_computation.2 | async-start | bytes 131072 | tf_op jit(solution)/shard_map/psum | solution.py:32
  65.6 83.0 %all-reduce.10.cloned.1.call-start = ((), (), s32[]{:S(2)}) async-start(), calls=%async_computation.3 | async-start | bytes 131072 | tf_op jit(solution)/shard_map/psum | solution.py:32
  115.3 83.0 %all-reduce.12.cloned.1.call-start = ((), (), s32[]{:S(2)}) async-start(), calls=%async_computation.4 | async-start | bytes 131072 | tf_op jit(solution)/shard_map/psum | solution.py:32
  165.0 83.0 %all-reduce.14.cloned.1.call-start = ((), (), s32[]{:S(2)}) async-start(), calls=%async_computation.5 | async-start | bytes 131072 | tf_op jit(solution)/shard_map/psum | solution.py:32
  214.1 50.5 %copy-start.3 = (s32[32]{0:T(128)S(1)}, s32[32]{0:T(128)}, u32[]{:S(2)}) copy-start(s32[32]{0:T(128)} %param.8) | copy-start | bytes 388
  214.1 69.4 %copy-start.2 = (f32[16,4,256]{2,1,0:T(4,128)S(1)}, f32[16,4,256]{2,1,0:T(4,128)}, u32[]{:S(2)}) copy-start(f32[16,4,256]{2,1,0:T(4,128)} %param.7) | copy-start | bytes 196612
  214.8 68.8 %reduce-scatter.2.cloned.1.call-start = ((), (), s32[]{:S(2)}) async-start(), calls=%async_computation.6 | async-start | bytes 327680 | tf_op jit(solution)/shard_map/reduce_scatter | solution.py:53
Sparse Core Ops, SparseCore 0:
  11.8 37.0 all-reduce.5
  65.7 33.0 all-reduce.7
  115.4 33.0 all-reduce.9
  165.2 33.0 all-reduce.11
  214.9 33.0 all-reduce.13
  264.7 18.7 reduce-scatter.1
where the time goes:
time: 293 us; the launch traced here: 292 us
  waiting for transfers between devices  178 us (61%)
  blocking collectives  60.6 us (21%)
  between operations  25.9 us (9%)
  matrix products  18.2 us (6%)
  other arithmetic  4.76 us (2%)
  local copies, waits for them, and re-layouts  4.48 us (2%)
    psum x5, waiting for transfers between devices, per_device(): remaining = lax.psum(placed - part_tile, 'row')  159 us
    psum x5, blocking collectives, spread(): return lax.psum(block, axis)  60.6 us
    reduce_scatter x1, waiting for transfers between devices, per_device(): lax.psum_scatter(shaped, 'row', scatter_dimension=2, tiled=True)  18.8 us
    dot_general x5, matrix products, per_device(): lax.dot_general(sent_block, panel_rows, (((1,), (1,)), ((), ())), preferr...  11.2 us
    dot_general x5, matrix products, per_device(): lax.dot_general(remaining, inverse, (((1,), (1,)), ((), ())), precision=l...  7.03 us
  transfers between devices with their start and end apart: 6, of which 6 were waited for; matrix products, arithmetic and copies ran while one was open for 0% of the time, Pallas kernels for 0%

commit v1 on v0

--- a/solution.py
+++ b/solution.py
@@ -29,7 +29,7 @@
         placed = lax.dynamic_update_slice_in_dim(
             jnp.zeros((rhs_count, tile_width), jnp.float32), rhs_slice, slice_start, 1
         )
-        remaining = lax.psum(placed - part_tile, "row")
+        remaining = jnp.sum(lax.all_gather(placed - part_tile, "row"), axis=0)
         inverse = diag_inverse[section].astype(jnp.float32)
         solved = lax.dot_general(
             remaining,

time: 293 us -> 203 us (0.69)
  waiting for transfers between devices: 178 us -> 20.9 us
  blocking collectives: 60.6 us -> 134 us
  matrix products: 18.2 us -> 14.8 us
    psum x5 -> x0, waiting for transfers between devices: 159 us -> none  [per_device(): remaining = lax.psum(placed - part_tile, 'row')]
    all_gather x0 -> x5, blocking collectives: none -> 73.2 us  [per_device(): remaining = jnp.sum(lax.all_gather(placed - part_tile, 'row'), axis=0)]
    dot_general x5, matrix products: 7.03 us -> 3.62 us  [per_device(): lax.dot_general(remaining, inverse, (((1,), (1,)), ((), ())), precision=l...]
  transfers between devices with their start and end apart: 6 -> 1, of which waited for: 6 -> 1; matrix products, arithmetic and copies ran while one was open for 0% -> 0% of each run, Pallas kernels for 0% -> 0%
where the time goes in v1:
time: 203 us; the launch traced here: 202 us
  blocking collectives  134 us (66%)
  between operations  26.4 us (13%)
  waiting for transfers between devices  20.9 us (10%)
  matrix products  14.8 us (7%)
  local copies, waits for them, and re-layouts  3.93 us (2%)
  other arithmetic  2.34 us (1%)
    all_gather x5, blocking collectives, per_device(): remaining = jnp.sum(lax.all_gather(placed - part_tile, 'row'), axis=0)  73.2 us
    psum x5, blocking collectives, spread(): return lax.psum(block, axis)  60.4 us
    reduce_scatter x1, waiting for transfers between devices, per_device(): lax.psum_scatter(shaped, 'row', scatter_dimension=2, tiled=True)  20.9 us
    dot_general x5, matrix products, per_device(): lax.dot_general(sent_block, panel_rows, (((1,), (1,)), ((), ())), preferr...  11.2 us
  transfers between devices with their start and end apart: 1, of which 1 were waited for; matrix products, arithmetic and copies ran while one was open for 0% of the time, Pallas kernels for 0%

profile of v1, /device:TPU:0, one launch (start us, length us, event | category | flops | bytes accessed | tf_op | source)
XLA Modules:
  0.0 202.1 jit_solution(2633194432038082420)
XLA Ops:
  6.5 1.5 fusion.35
  20.8 0.9 copy.30
  21.7 15.7 %all_gather.34 = f32[4,16,1024]{2,1,0:T(8,128)S(1)} all-gather(f32[1,16,1024]{2,1,0:T(8,128)S(1)} %bitcast_dynamic-update-slice_fusion.5), channel_id=1, replica_groups=mesh['row'=4,'col'=8] {'row'}, dimensions={0}, use_global_device_ids=true | all-gather | bytes 327680 | tf_op jit(solution)/shard_map/all_gather | solution.py:32
  37.4 0.7 broadcast_compare_fusion
  38.1 1.6 bitcast_dynamic-update-slice_fusion.4
  39.8 12.2 %psum.35 = bf16[16,256]{1,0:T(8,128)(2,1)S(1)} all-reduce(bf16[16,256]{1,0:T(8,128)(2,1)S(1)} %fusion.30), channel_id=1, replica_groups=mesh['row'=4,'col'=8] {'col'}, use_global_device_ids=true, to_apply=%region_2.3 | all-reduce | flops 4096 | bytes 16384 | tf_op jit(solution)/shard_map/psum | solution.py:9
  52.0 2.2 %fusion.4 = f32[16,4096]{1,0:T(8,128)S(1)} fusion(bf16[16,256]{1,0:T(8,128)(2,1)S(1)} %psum.35, bf16[4096,5,256]{2,0,1:T(8,128)(2,1)} %param.5), kind=kOutput, calls=%fused_computation.8 | convolution fusion | flops 33554432 | bytes 2367488 | tf_op jit(solution)/shard_map/dot_general | solution.py:49
  54.3 14.1 %all-gather = f32[64,1024]{1,0:T(8,128)S(1)} all-gather(f32[16,1024]{1,0:T(8,128)S(1)} %dynamic-slice_subtract_fusion.3), channel_id=2, replica_groups=mesh['row'=4,'col'=8] {'row'}, dimensions={0}, use_global_device_ids=true | all-gather | bytes 327680 | tf_op jit(solution)/shard_map/all_gather | solution.py:32
  69.0 12.1 %psum.36 = bf16[16,256]{1,0:T(8,128)(2,1)S(1)} all-reduce(bf16[16,256]{1,0:T(8,128)(2,1)S(1)} %fusion.31), channel_id=1, replica_groups=mesh['row'=4,'col'=8] {'col'}, use_global_device_ids=true, to_apply=%region_4.5 | all-reduce | flops 4096 | bytes 16384 | tf_op jit(solution)/shard_map/psum | solution.py:9
  81.1 2.2 %convolution_add_fusion.3 = f32[16,4096]{1,0:T(8,128)S(1)} fusion(f32[16,4096]{1,0:T(8,128)S(1)} %fusion.4, bf16[16,256]{1,0:T(8,128)(2,1)S(1)} %psum.36, bf16[4096,5,256]{2,0,1:T(8,128)(2,1)} %param.5), kind=kOutput, calls=%fused_computation.3 | convolution fusion | flops 33619968 | bytes 2629632 | tf_op jit(solution)/shard_map/dot_general | solution.py:49
  83.4 14.5 %all-gather.1 = f32[64,1024]{1,0:T(8,128)S(1)} all-gather(f32[16,1024]{1,0:T(8,128)S(1)} %dynamic-slice_subtract_fusion.2), channel_id=3, replica_groups=mesh['row'=4,'col'=8] {'row'}, dimensions={0}, use_global_device_ids=true | all-gather | bytes 327680 | tf_op jit(solution)/shard_map/all_gather | solution.py:32
  98.5 12.1 %psum.37 = bf16[16,256]{1,0:T(8,128)(2,1)S(1)} all-reduce(bf16[16,256]{1,0:T(8,128)(2,1)S(1)} %fusion.32), channel_id=1, replica_groups=mesh['row'=4,'col'=8] {'col'}, use_global_device_ids=true, to_apply=%region_6.7 | all-reduce | flops 4096 | bytes 16384 | tf_op jit(solution)/shard_map/psum | solution.py:9
  110.6 2.2 %convolution_add_fusion.2 = f32[16,4096]{1,0:T(8,128)S(1)} fusion(f32[16,4096]{1,0:T(8,128)S(1)} %convolution_add_fusion.3, bf16[16,256]{1,0:T(8,128)(2,1)S(1)} %psum.37, bf16[4096,5,256]{2,0,1:T(8,128)(2,1)} %param.5), kind=kOutput, calls=%fused_computation.2 | convolution fusion | flops 33619968 | bytes 2629632 | tf_op jit(solution)/shard_map/dot_general | solution.py:49
  112.9 14.5 %all-gather.2 = f32[64,1024]{1,0:T(8,128)S(1)} all-gather(f32[16,1024]{1,0:T(8,128)S(1)} %dynamic-slice_subtract_fusion.1), channel_id=4, replica_groups=mesh['row'=4,'col'=8] {'row'}, dimensions={0}, use_global_device_ids=true | all-gather | bytes 327680 | tf_op jit(solution)/shard_map/all_gather | solution.py:32
  127.4 0.5 fusion.27
  128.0 12.1 %psum.38 = bf16[16,256]{1,0:T(8,128)(2,1)S(1)} all-reduce(bf16[16,256]{1,0:T(8,128)(2,1)S(1)} %fusion.33), channel_id=1, replica_groups=mesh['row'=4,'col'=8] {'col'}, use_global_device_ids=true, to_apply=%region_8.9 | all-reduce | flops 4096 | bytes 16384 | tf_op jit(solution)/shard_map/psum | solution.py:9
  140.0 2.2 %convolution_add_fusion.1 = f32[16,4096]{1,0:T(8,128)S(1)} fusion(f32[16,4096]{1,0:T(8,128)S(1)} %convolution_add_fusion.2, bf16[16,256]{1,0:T(8,128)(2,1)S(1)} %psum.38, bf16[4096,5,256]{2,0,1:T(8,128)(2,1)} %param.5), kind=kOutput, calls=%fused_computation.1 | convolution fusion | flops 33619968 | bytes 2629632 | tf_op jit(solution)/shard_map/dot_general | solution.py:49
  142.4 14.5 %all-gather.3 = f32[64,1024]{1,0:T(8,128)S(1)} all-gather(f32[16,1024]{1,0:T(8,128)S(1)} %dynamic-slice_subtract_fusion), channel_id=5, replica_groups=mesh['row'=4,'col'=8] {'row'}, dimensions={0}, use_global_device_ids=true | all-gather | bytes 327680 | tf_op jit(solution)/shard_map/all_gather | solution.py:32
  157.5 12.1 %psum.39 = bf16[16,256]{1,0:T(8,128)(2,1)S(1)} all-reduce(bf16[16,256]{1,0:T(8,128)(2,1)S(1)} %fusion.34), channel_id=1, replica_groups=mesh['row'=4,'col'=8] {'col'}, use_global_device_ids=true, to_apply=%region_10.11 | all-reduce | flops 4096 | bytes 16384 | tf_op jit(solution)/shard_map/psum | solution.py:9
  169.5 2.2 %convolution_add_fusion = f32[16,4096]{1,0:T(8,128)S(1)} fusion(f32[16,4096]{1,0:T(8,128)S(1)} %convolution_add_fusion.1, bf16[16,256]{1,0:T(8,128)(2,1)S(1)} %psum.39, bf16[4096,5,256]{2,0,1:T(8,128)(2,1)} %param.5), kind=kOutput, calls=%fused_computation | convolution fusion | flops 33619968 | bytes 2629632 | tf_op jit(solution)/shard_map/dot_general | solution.py:49
  171.8 0.7 copy.41
  172.7 20.9 %reduce-scatter.2.cloned.1.call-done = f32[16,4,256]{2,0,1:T(8,128)} async-done(((f32[16,4,1024]{2,0,1:T(8,128)}), f32[16,4,256]{2,0,1:T(8,128)}) %reduce-scatter.2.cloned.1.call-update) | async-done | bytes 65552 | tf_op jit(solution)/shard_map/reduce_scatter | solution.py:53
  193.6 0.9 subtract_select_fusion
  194.5 0.7 copy.37
  (38 shorter events, 2.5 us)
Async XLA Ops:
  6.5 61.9 %copy-start = (bf16[5,256,1024]{2,1,0:T(8,128)(2,1)S(1)}, bf16[5,256,1024]{2,1,0:T(8,128)(2,1)}, u32[]{:S(2)}) copy-start(bf16[5,256,1024]{2,1,0:T(8,128)(2,1)} %param.6) | copy-start | bytes 7864324
  6.5 187.1 %reduce-scatter.2.cloned.1.call-start = ((), (), s32[]{:S(2)}) async-start(), calls=%async_computation.1 | async-start | bytes 327680 | tf_op jit(solution)/shard_map/reduce_scatter | solution.py:53
  142.3 30.2 %copy-start.2 = (s32[32]{0:T(128)S(1)}, s32[32]{0:T(128)}, u32[]{:S(2)}) copy-start(s32[32]{0:T(128)} %param.8) | copy-start | bytes 388
  142.3 51.3 %copy-start.1 = (f32[16,4,256]{2,1,0:T(4,128)S(1)}, f32[16,4,256]{2,1,0:T(4,128)}, u32[]{:S(2)}) copy-start(f32[16,4,256]{2,1,0:T(4,128)} %param.7) | copy-start | bytes 196612
Sparse Core Ops, SparseCore 0:
  172.6 20.9 reduce-scatter.1
